TPU v7x, 32 devices: a whole 2x2x4 slice. The times are simulated.
32 devices in a mesh: inst: 4 (over x, core), blk: 8 (over z, y).
Axes of the slice: x: 2, y: 2, z: 4, core: 2. Of those that a mesh axis runs over, the one named last changes fastest.
Arguments:
- state: float32 [16, 5, 16, 64, 256], P('inst', None, None, 'blk'), may hold values from -0.53 to 3.9, as said below
- multiples: int32 [7], replicated, may hold values from 1 to 4
Outputs:
- state_change: float32 [16, 5, 16, 64, 256], P('inst', None, None, 'blk')
Inputs may be any that keep to these rules, and one draw needn't show every extreme that they name: `state`: density and pressure lie in 0.7 to 1.3, the axial velocity in 0.2 to 0.8 and the other two velocity components in -0.4 to 0.4; the last variable is the total energy p / 0.4 + rho (u u + v v + w w) / 2.
All inputs are finite; a program needn't handle non-finite values.
Results may differ from a plain program's by a relative error of at most 0.0003.
Values sent between devices are 32-bit elements; how exact they have to be, the bound alone decides.
No kernel may reach another device: no remote copies, remote signals or barrier semaphores. Data moves between devices by JAX's collectives and lax.ppermute only.
A program may use at most 128 MiB of HBM per device.

v0:
```python
import math

import jax
import jax.numpy as jnp
from jax import lax
from jax.sharding import PartitionSpec as P

NT = 16


heat_ratio = 1.4
segment_step = 0.05
smooth_weight = 0.5
base_rate = 0.5
diagonal_weight = 3.0


def extended_2(cells, sides, width):
    for axis, dim in sides:
        count = lax.axis_size(axis)
        head = lax.slice_in_dim(cells, 0, width, axis=dim)
        tail = lax.slice_in_dim(cells, cells.shape[dim] - width, cells.shape[dim], axis=dim)
        cells = jnp.concatenate(
            [
                lax.ppermute(tail, axis, [(i, (i + 1) % count) for i in range(count)]),
                cells,
                lax.ppermute(head, axis, [((i + 1) % count, i) for i in range(count)]),
            ],
            axis=dim,
        )
    return cells


def limited(lower, upper):
    return jnp.maximum(0.0, jnp.minimum(lower, upper)) + jnp.minimum(0.0, jnp.maximum(lower, upper))


def take_part(array_in, offset, amount, along):
    return lax.slice_in_dim(array_in, offset, offset + amount, axis=along)


def primitive(conserved):
    density = conserved[:, 0]
    velocity = [conserved[:, 1] / density, conserved[:, 2] / density, conserved[:, 3] / density]
    kinetic = (
        0.5
        * density
        * (velocity[0] * velocity[0] + velocity[1] * velocity[1] + velocity[2] * velocity[2])
    )
    pressure = (heat_ratio - 1.0) * (conserved[:, 4] - kinetic)
    return [density] + velocity + [pressure]


def physical(states, normal):
    density = states[0]
    pressure = states[4]
    velocity = states[1:4]
    normal_speed = velocity[normal]
    energy = pressure / (heat_ratio - 1.0) + 0.5 * density * (
        velocity[0] * velocity[0] + velocity[1] * velocity[1] + velocity[2] * velocity[2]
    )
    conserved = [
        density,
        density * velocity[0],
        density * velocity[1],
        density * velocity[2],
        energy,
    ]
    flux = [density * normal_speed]
    for member in range(3):
        momentum = density * normal_speed * velocity[member]
        if member == normal:
            momentum = momentum + pressure
        flux.append(momentum)
    flux.append((energy + pressure) * normal_speed)
    wave_speed = jnp.abs(normal_speed) + jnp.sqrt(heat_ratio * pressure / density)
    return (flux, conserved, wave_speed)


def divergence(states, along, normal):
    extent = states[0].shape[along]
    interior = extent - 4
    left_side = []
    right_side = []
    for component in states:
        differences = take_part(component, 1, extent - 1, along) - take_part(
            component, 0, extent - 1, along
        )
        slopes = limited(
            take_part(differences, 0, interior + 2, along),
            take_part(differences, 1, interior + 2, along),
        )
        centres = take_part(component, 1, interior + 2, along)
        left_side.append(
            take_part(centres, 0, interior + 1, along)
            + 0.5 * take_part(slopes, 0, interior + 1, along)
        )
        right_side.append(
            take_part(centres, 1, interior + 1, along)
            - 0.5 * take_part(slopes, 1, interior + 1, along)
        )
    left_flux, left_cons, left_speed = physical(left_side, normal)
    right_flux, right_cons, right_speed = physical(right_side, normal)
    wave_speed = jnp.maximum(left_speed, right_speed)
    result = []
    for member in range(5):
        face_flux = 0.5 * (left_flux[member] + right_flux[member]) - 0.5 * wave_speed * (
            right_cons[member] - left_cons[member]
        )
        result.append(
            take_part(face_flux, 1, interior, along) - take_part(face_flux, 0, interior, along)
        )
    return result


def residual(extended):
    states = primitive(extended)
    inner = [component[:, :, 2:-2, :] for component in states]
    circum = divergence(states, 2, 1)
    axial = divergence(
        [jnp.pad(component, ((0, 0), (2, 2), (0, 0), (0, 0)), mode="edge") for component in inner],
        1,
        0,
    )
    radial = divergence(
        [jnp.pad(component, ((0, 0), (0, 0), (0, 0), (2, 2)), mode="edge") for component in inner],
        3,
        2,
    )
    return jnp.stack(
        [axial[member] + circum[member] + radial[member] for member in range(5)], axis=1
    )


def transform_tables(instances):
    indices = jnp.arange(instances, dtype=jnp.int32)
    harmonic = jnp.where(indices < 2, indices * (instances // 2), indices // 2)
    phases = harmonic[:, None] * indices[None, :] % instances
    angles = phases.astype(jnp.float32) * (2.0 * math.pi / instances)
    sine_rows = (indices % 2 == 1) & (indices >= 2)
    basis = jnp.where(sine_rows[:, None], jnp.sin(angles), jnp.cos(angles))
    weights = jnp.where(indices < 2, 1.0 / instances, 2.0 / instances).astype(jnp.float32)
    return (basis * weights[:, None], basis.T)


def pair_solve(right, frequency):
    cosine_part = right[:, 0]
    sine_part = right[:, 1]
    determinant = diagonal_weight * diagonal_weight + frequency * frequency
    return jnp.stack(
        [
            (diagonal_weight * cosine_part - frequency * sine_part) / determinant,
            (diagonal_weight * sine_part + frequency * cosine_part) / determinant,
        ],
        axis=1,
    )


def neighbours(extended):
    circum = extended[:, :, :, :, :-2] + extended[:, :, :, :, 2:]
    middle = extended[:, :, :, :, 1:-1]
    padded = jnp.pad(middle, ((0, 0), (0, 0), (0, 0), (0, 0), (0, 0), (1, 1)))
    return circum + (padded[:, :, :, :, :, :-2] + padded[:, :, :, :, :, 2:])


def body(state, multiples):
    extended = extended_2(state, (("blk", 3),), 2)
    first_sweep = residual(extended)
    segmented = state - segment_step * first_sweep
    segmented_ext = extended_2(segmented, (("blk", 3),), 2)
    second_sweep = residual(segmented_ext)
    state_freq, residual_freq = (
        lax.all_to_all(state, "inst", split_axis=2, concat_axis=0, tiled=True),
        lax.all_to_all(second_sweep, "inst", split_axis=2, concat_axis=0, tiled=True),
    )
    forward, inverse = transform_tables(NT)
    layout = residual_freq.shape
    paired = (NT // 2, 2) + layout[1:]
    residual_hat = jnp.dot(
        forward, residual_freq.reshape(NT, -1), precision=lax.Precision.HIGHEST
    ).reshape(paired)
    state_hat = jnp.dot(
        forward, state_freq.reshape(NT, -1), precision=lax.Precision.HIGHEST
    ).reshape(paired)
    frequency = jnp.concatenate(
        [jnp.zeros((1,), jnp.float32), base_rate * multiples.astype(jnp.float32)]
    ).reshape(NT // 2, 1, 1, 1, 1)
    source = jnp.stack([frequency * state_hat[:, 1], -frequency * state_hat[:, 0]], axis=1)
    right_hand = -(residual_hat + source)
    widened = extended_2(right_hand, (("blk", 4),), 3)
    correction = pair_solve(widened, frequency)
    for repeat in range(3):
        trimmed = lax.slice_in_dim(widened, repeat + 1, widened.shape[4] - repeat - 1, axis=4)
        correction = pair_solve(trimmed + smooth_weight * neighbours(correction), frequency)
    change_freq = jnp.dot(
        inverse, correction.reshape(NT, -1), precision=lax.Precision.HIGHEST
    ).reshape(layout)
    return lax.all_to_all(change_freq, "inst", split_axis=0, concat_axis=2, tiled=True)


def solution(mesh):
    return jax.shard_map(
        body,
        mesh=mesh,
        in_specs=(P("inst", None, None, "blk", None), P()),
        out_specs=P("inst", None, None, "blk", None),
        check_vma=False,
    )
```

profile of v0, /device:TPU:0, one launch (start us, length us, event | category | flops | bytes accessed | tf_op | source)
XLA Modules:
  0.0 393.6 jit_solution(17723114507473512996)
XLA Ops:
  0.0 3.2 fusion.217
  3.2 3.0 collective-permute-start
  6.2 3.1 collective-permute-start.1
  9.3 24.9 %collective-permute-done = f32[4,5,16,2,256]{4,3,0,2,1:T(2,128)S(1)} collective-permute-done((f32[4,5,16,2,256]{4,3,0,2,1:T(2,128)S(1)}, f32[4,5,16,2,256]{4,3,0,2,1:T(2,128)S(1)}, u32[]{:S(2)}, u32[]{:S(2)}) %collective-permute-start) | collective-permute-done | bytes 655392 | tf_op jit(solution)/shard_map/ppermute | solution.py:25
  34.3 2.2 collective-permute-done.1
  40.3 2.7 multiply_subtract_fusion.26
  94.1 4.4 %multiply_subtract_fusion.16 = (f32[4,16,8,257]{3,2,0,1:T(8,128)S(1)}, f32[4,16,8,257]{3,2,0,1:T(8,128)S(1)}, f32[4,16,8,257]{3,2,0,1:T(8,128)S(1)}, f32[4,16,8,257]{3,2,0,1:T(8,128)S(1)}, f32[4,16,8,257]{3,2,0,1:T(8,128)S(1)}) fusion(f32[4,16,8,258]{3,2,0,1:T(8,128)S(1)} %copy-done.26, f32[4,16,8,256]{3,2,0,1:T(8,128)S(1)} %copy-done.34, ...), kind=kLoop, calls=%fused_computation.254 | loop fusion | flops 8816128 | bytes 10557440 | tf_op jit(solution)/shard_map/sub | solution.py:107
  107.7 3.5 multiply_subtract_fusion.6
  111.3 2.4 multiply_subtract_fusion.7
  119.6 4.4 %collective-permute-start.3 = (f32[4,5,16,2,256]{4,3,0,2,1:T(2,128)}, f32[4,5,16,2,256]{4,3,0,2,1:T(2,128)}, u32[]{:S(2)}, u32[]{:S(2)}) collective-permute-start(f32[4,5,16,2,256]{4,3,0,2,1:T(2,128)} %get-tuple-element.74), channel_id=1, source_target_pairs={{1,0},{2,1},{3,2},{4,3},{5,4},{6,5},{7,6},{0,7},{9,8},{10,9},{11,1... | collective-permute-start | bytes 1966088 | tf_op jit(solution)/shard_map/ppermute | solution.py:27
  125.8 4.5 %all-to-all-start.1 = ((f32[4,5,16,8,256]{4,3,1,0,2:T(8,128)}), f32[4,5,16,8,256]{4,3,1,0,2:T(8,128)}, u32[]{:S(2)}, u32[]{:S(2)}) async-start(f32[4,5,16,8,256]{4,3,1,0,2:T(8,128)} %copy.120), calls=%async_computation.1 | async-start | bytes 5242880 | tf_op jit(solution)/shard_map/all_to_all | solution.py:173
  130.4 16.7 %collective-permute-done.2 = f32[4,5,16,2,256]{4,3,0,2,1:T(2,128)S(1)} collective-permute-done((f32[4,5,16,2,256]{4,3,0,2,1:T(2,128)}, f32[4,5,16,2,256]{4,3,0,2,1:T(2,128)S(1)}, u32[]{:S(2)}, u32[]{:S(2)}) %collective-permute-start.2) | collective-permute-done | bytes 655392 | tf_op jit(solution)/shard_map/ppermute | solution.py:25
  147.1 3.9 collective-permute-done.3
  151.0 2.1 pad_maximum_fusion.1
  161.3 2.4 multiply_subtract_fusion.21
  217.6 4.3 %multiply_subtract_fusion.11 = (f32[4,16,8,257]{3,2,0,1:T(8,128)S(1)}, f32[4,16,8,257]{3,2,0,1:T(8,128)S(1)}, f32[4,16,8,257]{3,2,0,1:T(8,128)S(1)}, f32[4,16,8,257]{3,2,0,1:T(8,128)S(1)}, f32[4,16,8,257]{3,2,0,1:T(8,128)S(1)}) fusion(f32[4,16,8,258]{3,2,0,1:T(8,128)S(1)} %minimum_add_fusion.11, f32[4,16,8,256]{3,2,0,1:T(8,128)S(1)} %copy-done.32, ...), kind=kLoop, calls=%fused_computation.243 | loop fusion | flops 8816128 | bytes 10557440 | tf_op jit(solution)/shard_map/sub | solution.py:107
  228.8 4.3 %multiply_subtract_fusion.1 = (f32[4,16,9,256]{3,2,0,1:T(8,128)S(1)}, f32[4,16,9,256]{3,2,0,1:T(8,128)S(1)}, f32[4,16,9,256]{3,2,0,1:T(8,128)S(1)}, f32[4,16,9,2...) fusion(f32[4,16,10,256]{3,2,0,1:T(8,128)S(1)} %minimum_add_fusion.1, ...), kind=kLoop, calls=%fused_computation.141 | loop fusion | flops 8404992 | bytes 15335424 | tf_op jit(solution)/shard_map/sub | solution.py:107
  233.1 3.3 multiply_subtract_fusion.2
  244.9 4.0 %all-to-all-start = ((f32[4,5,16,8,256]{4,3,0,1,2:T(8,128)}), f32[4,5,16,8,256]{4,3,0,1,2:T(8,128)S(1)}, u32[]{:S(2)}, u32[]{:S(2)}) async-start(f32[4,5,16,8,256]{4,3,0,1,2:T(8,128)} %copy.116), calls=%async_computation | async-start | bytes 5242880 | tf_op jit(solution)/shard_map/all_to_all | solution.py:174
  249.0 3.6 copy.151
  252.6 3.1 reshape.409
  255.7 2.5 copy.131
  258.2 3.7 fusion.22
  261.8 2.0 slice_multiply_fusion.1
  263.9 16.2 %all-to-all-done = f32[4,5,16,8,256]{4,3,0,1,2:T(8,128)S(1)} async-done(((f32[4,5,16,8,256]{4,3,0,1,2:T(8,128)}), f32[4,5,16,8,256]{4,3,0,1,2:T(8,128)S(1)}, u32[]{:S(2)}, u32[]{:S(2)}) %all-to-all-start) | async-done | bytes 2621472 | tf_op jit(solution)/shard_map/all_to_all | solution.py:174
  285.6 3.9 fusion.21
  289.8 4.9 %collective-permute-start.5 = (f32[8,2,5,4,3,256]{5,0,4,3,2,1:T(8,128)S(1)}, f32[8,2,5,4,3,256]{5,0,4,3,2,1:T(8,128)S(1)}, u32[]{:S(2)}, u32[]{:S(2)}) collective-permute-start(f32[8,2,5,4,3,256]{5,0,4,3,2,1:T(8,128)S(1)} %get-tuple-element.72), channel_id=1, source_target_pairs={{1,0},{2,1},{3,2},{4,3},{5,4},{6,5},{7,6},{0,7},{9,8},{10,9},{11,1... | collective-permute-start | bytes 2949128 | tf_op jit(solution)/shard_map/ppermute | solution.py:27
  294.8 37.1 %collective-permute-done.4 = f32[8,2,5,4,3,256]{5,0,4,3,2,1:T(8,128)S(1)} collective-permute-done((f32[8,2,5,4,3,256]{5,0,4,3,2,1:T(8,128)S(1)}, f32[8,2,5,4,3,256]{5,0,4,3,2,1:T(8,128)S(1)}, u32[]{:S(2)}, u32[]{:S(2)}) %collective-permute-start.4) | collective-permute-done | bytes 983072 | tf_op jit(solution)/shard_map/ppermute | solution.py:25
  331.9 3.3 collective-permute-done.5
  350.0 2.5 copy.132
  352.6 3.6 fusion.26
  357.7 33.8 %all_to_all.48 = f32[16,5,4,8,256]{4,3,2,1,0:T(8,128)S(1)} all-to-all(f32[16,5,4,8,256]{4,3,2,1,0:T(8,128)S(1)} %copy.125), channel_id=1, replica_groups=mesh['inst'=4,'blk'=8] {'inst'}, dimensions={0} | all-to-all | bytes 5242880 | tf_op jit(solution)/shard_map/all_to_all | solution.py:198
  (454 shorter events, 171.3 us)
Async XLA Ops:
  0.0 36.5 %copy-start.18 = (f32[4,5,16,8,256]{4,3,2,1,0:T(8,128)S(1)}, f32[4,5,16,8,256]{4,3,2,1,0:T(8,128)}, u32[]{:S(2)}) copy-start(f32[4,5,16,8,256]{4,3,2,1,0:T(8,128)} %param.2) | copy-start | bytes 7864324
  3.2 31.1 %collective-permute-start = (f32[4,5,16,2,256]{4,3,0,2,1:T(2,128)S(1)}, f32[4,5,16,2,256]{4,3,0,2,1:T(2,128)S(1)}, u32[]{:S(2)}, u32[]{:S(2)}) collective-permute-start(f32[4,5,16,2,256]{4,3,0,2,1:T(2,128)S(1)} %get-tuple-element.75), channel_id=1, source_target_pairs={{0,1},{1,2},{2,3},{3,4},{4,5},{5,6},{6,7},{7,0},{8,9},{9,10},{10,1... | collective-permute-start | bytes 1966088 | tf_op jit(solution)/shard_map/ppermute | solution.py:25
  6.2 30.2 %collective-permute-start.1 = (f32[4,5,16,2,256]{4,3,0,2,1:T(2,128)S(1)}, f32[4,5,16,2,256]{4,3,0,2,1:T(2,128)S(1)}, u32[]{:S(2)}, u32[]{:S(2)}) collective-permute-start(f32[4,5,16,2,256]{4,3,0,2,1:T(2,128)S(1)} %get-tuple-element.76), channel_id=1, source_target_pairs={{1,0},{2,1},{3,2},{4,3},{5,4},{6,5},{7,6},{0,7},{9,8},{10,9},{11,1... | collective-permute-start | bytes 1966088 | tf_op jit(solution)/shard_map/ppermute | solution.py:27
  38.3 9.0 %copy-start.10 = (f32[4,16,12,256]{3,2,0,1:T(8,128)}, f32[4,16,12,256]{3,2,0,1:T(8,128)S(1)}, u32[]{:S(2)}) copy-start(f32[4,16,12,256]{3,2,0,1:T(8,128)S(1)} %get-tuple-element.45) | copy-start | bytes 2359300
  38.4 4.5 %copy-start.29 = (f32[4,16,8,256]{3,2,0,1:T(8,128)}, f32[4,16,8,256]{3,2,0,1:T(8,128)S(1)}, u32[]{:S(2)}) copy-start(f32[4,16,8,256]{3,2,0,1:T(8,128)S(1)} %slice.1936) | copy-start | bytes 1572868
  38.5 6.1 %copy-start.22 = (f32[4,16,8,256]{3,2,0,1:T(8,128)}, f32[4,16,8,256]{3,2,0,1:T(8,128)S(1)}, u32[]{:S(2)}) copy-start(f32[4,16,8,256]{3,2,0,1:T(8,128)S(1)} %slice.1978) | copy-start | bytes 1572868
  38.6 6.0 %copy-start.4 = (f32[4,16,8,256]{3,2,0,1:T(8,128)}, f32[4,16,8,256]{3,2,0,1:T(8,128)S(1)}, u32[]{:S(2)}) copy-start(f32[4,16,8,256]{3,2,0,1:T(8,128)S(1)} %slice.1892) | copy-start | bytes 1572868
  38.9 9.7 %copy-start.14 = (f32[4,16,12,256]{3,2,0,1:T(8,128)}, f32[4,16,12,256]{3,2,0,1:T(8,128)S(1)}, u32[]{:S(2)}) copy-start(f32[4,16,12,256]{3,2,0,1:T(8,128)S(1)} %slice_bitcast_fusion.9) | copy-start | bytes 2359300
  39.2 5.4 %copy-start.8 = (f32[4,18,8,256]{3,2,0,1:T(8,128)}, f32[4,18,8,256]{3,2,0,1:T(8,128)S(1)}, u32[]{:S(2)}) copy-start(f32[4,18,8,256]{3,2,0,1:T(8,128)S(1)} %minimum_add_fusion.27) | copy-start | bytes 1769476
  88.3 4.1 %copy-start.89 = (f32[4,16,8,2]{3,2,0,1:T(8,128)S(1)}, f32[4,16,8,2]{3,2,0,1:T(8,128)}, u32[]{:S(2)}) copy-start(f32[4,16,8,2]{3,2,0,1:T(8,128)} %copy-done.88) | copy-start | bytes 12292
  89.3 3.2 copy-start.87
  119.3 27.8 %collective-permute-start.2 = (f32[4,5,16,2,256]{4,3,0,2,1:T(2,128)}, f32[4,5,16,2,256]{4,3,0,2,1:T(2,128)S(1)}, u32[]{:S(2)}, u32[]{:S(2)}) collective-permute-start(f32[4,5,16,2,256]{4,3,0,2,1:T(2,128)} %get-tuple-element.73), channel_id=1, source_target_pairs={{0,1},{1,2},{2,3},{3,4},{4,5},{5,6},{6,7},{7,0},{8,9},{9,10},{10,1... | collective-permute-start | bytes 1966088 | tf_op jit(solution)/shard_map/ppermute | solution.py:25
  119.6 31.4 %collective-permute-start.3 = (f32[4,5,16,2,256]{4,3,0,2,1:T(2,128)}, f32[4,5,16,2,256]{4,3,0,2,1:T(2,128)}, u32[]{:S(2)}, u32[]{:S(2)}) collective-permute-start(f32[4,5,16,2,256]{4,3,0,2,1:T(2,128)} %get-tuple-element.74), channel_id=1, source_target_pairs={{1,0},{2,1},{3,2},{4,3},{5,4},{6,5},{7,6},{0,7},{9,8},{10,9},{11,1... | collective-permute-start | bytes 1966088 | tf_op jit(solution)/shard_map/ppermute | solution.py:27
  125.8 119.0 %all-to-all-start.1 = ((f32[4,5,16,8,256]{4,3,1,0,2:T(8,128)}), f32[4,5,16,8,256]{4,3,1,0,2:T(8,128)}, u32[]{:S(2)}, u32[]{:S(2)}) async-start(f32[4,5,16,8,256]{4,3,1,0,2:T(8,128)} %copy.120), calls=%async_computation.1 | async-start | bytes 5242880 | tf_op jit(solution)/shard_map/all_to_all | solution.py:173
  153.3 18.6 %copy-start.16 = (f32[4,16,12,256]{3,2,0,1:T(8,128)}, f32[4,16,12,256]{3,2,0,1:T(8,128)S(1)}, u32[]{:S(2)}) copy-start(f32[4,16,12,256]{3,2,0,1:T(8,128)S(1)} %slice_bitcast_fusion.4) | copy-start | bytes 2359300
  153.4 7.6 %copy-start.37 = (f32[4,16,8,256]{3,2,0,1:T(8,128)}, f32[4,16,8,256]{3,2,0,1:T(8,128)S(1)}, u32[]{:S(2)}) copy-start(f32[4,16,8,256]{3,2,0,1:T(8,128)S(1)} %slice.2032) | copy-start | bytes 1572868
  154.3 16.5 %copy-start.12 = (f32[4,16,12,256]{3,2,0,1:T(8,128)}, f32[4,16,12,256]{3,2,0,1:T(8,128)S(1)}, u32[]{:S(2)}) copy-start(f32[4,16,12,256]{3,2,0,1:T(8,128)S(1)} %get-tuple-element.25) | copy-start | bytes 2359300
  154.4 6.6 %copy-start.31 = (f32[4,16,8,256]{3,2,0,1:T(8,128)}, f32[4,16,8,256]{3,2,0,1:T(8,128)S(1)}, u32[]{:S(2)}) copy-start(f32[4,16,8,256]{3,2,0,1:T(8,128)S(1)} %slice.2041) | copy-start | bytes 1572868
  154.5 10.8 %copy-start.2 = (f32[4,16,8,256]{3,2,0,1:T(8,128)}, f32[4,16,8,256]{3,2,0,1:T(8,128)S(1)}, u32[]{:S(2)}) copy-start(f32[4,16,8,256]{3,2,0,1:T(8,128)S(1)} %slice.2054) | copy-start | bytes 1572868
  154.6 6.4 %copy-start.27 = (f32[4,16,8,256]{3,2,0,1:T(8,128)}, f32[4,16,8,256]{3,2,0,1:T(8,128)S(1)}, u32[]{:S(2)}) copy-start(f32[4,16,8,256]{3,2,0,1:T(8,128)S(1)} %slice.2098) | copy-start | bytes 1572868
  154.7 9.0 %copy-start.20 = (f32[4,16,8,256]{3,2,0,1:T(8,128)}, f32[4,16,8,256]{3,2,0,1:T(8,128)S(1)}, u32[]{:S(2)}) copy-start(f32[4,16,8,256]{3,2,0,1:T(8,128)S(1)} %slice.2140) | copy-start | bytes 1572868
  160.4 4.9 %copy-start.6 = (f32[4,18,8,256]{3,2,0,1:T(8,128)}, f32[4,18,8,256]{3,2,0,1:T(8,128)S(1)}, u32[]{:S(2)}) copy-start(f32[4,18,8,256]{3,2,0,1:T(8,128)S(1)} %minimum_add_fusion.22) | copy-start | bytes 1769476
  170.7 4.1 %copy-start.102 = (f32[4,16,8,1]{3,2,0,1:T(8,128)S(1)}, f32[4,16,8,1]{3,2,0,1:T(8,128)}, u32[]{:S(2)}) copy-start(f32[4,16,8,1]{3,2,0,1:T(8,128)} %get-tuple-element.90) | copy-start | bytes 6148
  176.7 4.5 %copy-start.90 = (f32[4,16,8,2]{3,2,0,1:T(8,128)}, f32[4,16,8,2]{3,2,0,1:T(8,128)S(1)}, u32[]{:S(2)}) copy-start(f32[4,16,8,2]{3,2,0,1:T(8,128)S(1)} %reshape.394) | copy-start | bytes 12292
  185.9 4.5 %copy-start.94 = (f32[4,16,8,2]{3,2,0,1:T(8,128)}, f32[4,16,8,2]{3,2,0,1:T(8,128)S(1)}, u32[]{:S(2)}) copy-start(f32[4,16,8,2]{3,2,0,1:T(8,128)S(1)} %reshape.396) | copy-start | bytes 12292
  211.8 4.1 %copy-start.93 = (f32[4,16,8,2]{3,2,0,1:T(8,128)S(1)}, f32[4,16,8,2]{3,2,0,1:T(8,128)}, u32[]{:S(2)}) copy-start(f32[4,16,8,2]{3,2,0,1:T(8,128)} %copy-done.92) | copy-start | bytes 12292
  212.8 3.2 copy-start.91
  233.1 3.3 copy-start.77
  244.8 4.0 %copy-start.103 = (s32[7]{0:T(128)S(1)}, s32[7]{0:T(128)}, u32[]{:S(2)}) copy-start(s32[7]{0:T(128)} %param.3) | copy-start | bytes 88
  244.9 35.2 %all-to-all-start = ((f32[4,5,16,8,256]{4,3,0,1,2:T(8,128)}), f32[4,5,16,8,256]{4,3,0,1,2:T(8,128)S(1)}, u32[]{:S(2)}, u32[]{:S(2)}) async-start(f32[4,5,16,8,256]{4,3,0,1,2:T(8,128)} %copy.116), calls=%async_computation | async-start | bytes 5242880 | tf_op jit(solution)/shard_map/all_to_all | solution.py:174
  289.8 42.1 %collective-permute-start.4 = (f32[8,2,5,4,3,256]{5,0,4,3,2,1:T(8,128)S(1)}, f32[8,2,5,4,3,256]{5,0,4,3,2,1:T(8,128)S(1)}, u32[]{:S(2)}, u32[]{:S(2)}) collective-permute-start(f32[8,2,5,4,3,256]{5,0,4,3,2,1:T(8,128)S(1)} %get-tuple-element.71), channel_id=1, source_target_pairs={{0,1},{1,2},{2,3},{3,4},{4,5},{5,6},{6,7},{7,0},{8,9},{9,10},{10,1... | collective-permute-start | bytes 2949128 | tf_op jit(solution)/shard_map/ppermute | solution.py:25
  289.8 45.3 %collective-permute-start.5 = (f32[8,2,5,4,3,256]{5,0,4,3,2,1:T(8,128)S(1)}, f32[8,2,5,4,3,256]{5,0,4,3,2,1:T(8,128)S(1)}, u32[]{:S(2)}, u32[]{:S(2)}) collective-permute-start(f32[8,2,5,4,3,256]{5,0,4,3,2,1:T(8,128)S(1)} %get-tuple-element.72), channel_id=1, source_target_pairs={{1,0},{2,1},{3,2},{4,3},{5,4},{6,5},{7,6},{0,7},{9,8},{10,9},{11,1... | collective-permute-start | bytes 2949128 | tf_op jit(solution)/shard_map/ppermute | solution.py:27
  (80 other events, 123.6 us)
where the time goes:
time: 400 us; the launch traced here: 394 us
  local copies, waits for them, and re-layouts  113 us (28%)
  waiting for transfers between devices  104 us (26%)
  other arithmetic  104 us (26%)
  blocking collectives  33.8 us (8%)
  starting transfers between devices  24.3 us (6%)
  matrix products  11.2 us (3%)
    ppermute x3, waiting for transfers between devices, extended_2(): lax.ppermute(tail, axis, [(i, (i + 1) % count) for i in range(count)])  78.8 us
    slice x48, local copies, waits for them, and re-layouts, residual(): jnp.pad(component, ((0, 0), (0, 0), (0, 0), (2, 2)), mode='edge')  44.3 us
    sub x20, other arithmetic, divergence(): 0.5 * (left_flux[member] + right_flux[member])  44 us
    all_to_all x1, blocking collectives, body(): lax.all_to_all(change_freq, 'inst', split_axis=0, concat_axis=2, tiled=True)  33.8 us
    unnamed x212, local copies, waits for them, and re-layouts  26.6 us
    reshape x20, local copies, waits for them, and re-layouts, residual(): jnp.pad(component, ((0, 0), (0, 0), (0, 0), (2, 2)), mode='edge')  17.8 us
    all_to_all x1, waiting for transfers between devices, body(): lax.all_to_all(second_sweep, 'inst', split_axis=2, concat_axis=0, tiled=T...  16.2 us
    concatenate x10, other arithmetic, residual(): jnp.pad(component, ((0, 0), (0, 0), (0, 0), (2, 2)), mode='edge')  14.2 us
  transfers between devices with their start and end apart: 8, of which 7 were waited for; matrix products, arithmetic and copies ran while one was open for 25% of the time, Pallas kernels for 0%

commit v1 on v0

v1 whole, which is shorter than its diff:
```python
import math
from functools import partial

import jax
import jax.numpy as jnp
from jax import lax
from jax.experimental import pallas as pl
from jax.experimental.pallas import tpu as pltpu
from jax.sharding import PartitionSpec as P


heat_ratio = 1.4
segment_step = 0.05
smooth_weight = 0.5
base_rate = 0.5
diagonal_weight = 3.0
sweeps = 3
SUB, LANE = 8, 128


def minmod(a, b):
    return jnp.maximum(jnp.minimum(a, b), jnp.minimum(0.0, jnp.maximum(a, b)))


def primitive(q):
    inverse = 1.0 / q[0]
    u, v, w = q[1] * inverse, q[2] * inverse, q[3] * inverse
    kinetic = 0.5 * (q[1] * u + q[2] * v + q[3] * w)
    return [q[0], u, v, w, (heat_ratio - 1.0) * (q[4] - kinetic)]


def physical(s, normal):
    rho, p = s[0], s[4]
    vel = s[1:4]
    mom = [rho * c for c in vel]
    energy = p * (1.0 / (heat_ratio - 1.0)) + 0.5 * (mom[0] * vel[0] + mom[1] * vel[1] + mom[2] * vel[2])
    un, m = vel[normal], mom[normal]
    flux = [m]
    for i in range(3):
        f = m * vel[i]
        flux.append(f + p if i == normal else f)
    flux.append((energy + p) * un)
    gp = heat_ratio * p
    speed = jnp.abs(un) + gp * lax.rsqrt(gp * rho)
    return flux, [rho] + mom + [energy], speed


def face(left, right):
    fl, ql, al = left
    fr, qr, ar = right
    a = jnp.maximum(al, ar)
    return [(fl[i] + fr[i]) - a * (qr[i] - ql[i]) for i in range(5)]


class Shift:
    def __init__(self, axis):
        self.axis = axis
        self.size = (SUB, LANE)[axis]
        pos = lax.broadcasted_iota(jnp.int32, (SUB, LANE), axis)
        self.first = pos == 0
        self.last = pos == self.size - 1

    def down(self, pieces):
        rolled = [pltpu.roll(a, 1, self.axis) for a in pieces]
        edge = [pieces[0]] + rolled[:-1]
        return [jnp.where(self.first, e, r) for e, r in zip(edge, rolled)]

    def up(self, pieces, end=None):
        rolled = [pltpu.roll(a, self.size - 1, self.axis) for a in pieces]
        edge = rolled[1:] + [pieces[-1] if end is None else end]
        return [jnp.where(self.last, e, r) for e, r in zip(edge, rolled)]


def line_divergence(W, shift, normal):
    count = len(W[0])
    plus, minus = [], []
    for v in range(5):
        ahead = shift.up(W[v])
        d = [0.5 * (a - w) for a, w in zip(ahead, W[v])]
        rolled = [pltpu.roll(x, 1, shift.axis) for x in d]
        edge = [jnp.zeros_like(d[0])] + rolled[:-1]
        back = [jnp.where(shift.first, e, r) for e, r in zip(edge, rolled)]
        s = [minmod(x, y) for x, y in zip(back, d)]
        plus.append(shift.down([w + x for w, x in zip(W[v], s)]))
        minus.append([w - x for w, x in zip(W[v], s)])
    low, ends = [], None
    for i in range(count):
        left = physical([plus[v][i] for v in range(5)], normal)
        right = physical([minus[v][i] for v in range(5)], normal)
        low.append(face(left, right))
        ends = right[0]
    out = []
    for v in range(5):
        mine = [low[i][v] for i in range(count)]
        nxt = shift.up(mine, end=ends[v] + ends[v])
        out.append([b - a for a, b in zip(mine, nxt)])
    return out


def tiles(X, Z):
    return [(t, h) for t in range(X // SUB) for h in range(Z // LANE)]


def at(t, h):
    return pl.ds(t * SUB, SUB), pl.ds(h * LANE, LANE)


def xz_kernel(first, *refs):
    if first:
        src, prim, base, split = refs
    else:
        src, base = refs
        prim = src
    _, _, Y, X, Z = src.shape
    sx, sz = Shift(0), Shift(1)

    def row(y, carry):
        if first:
            for t, h in tiles(X, Z):
                r, c = at(t, h)
                q = [src[0, v, y, r, c] for v in range(5)]
                w = primitive(q)
                for v in range(5):
                    prim[0, v, y, r, c] = w[v]
        for h in range(Z // LANE):
            W = [[prim[0, v, y, at(t, h)[0], at(t, h)[1]] for t in range(X // SUB)] for v in range(5)]
            div = line_divergence(W, sx, 0)
            for t in range(X // SUB):
                r, c = at(t, h)
                for v in range(5):
                    base[0, v, y, r, c] = div[v][t]
        for t in range(X // SUB):
            W = [[prim[0, v, y, at(t, h)[0], at(t, h)[1]] for h in range(Z // LANE)] for v in range(5)]
            div = line_divergence(W, sz, 2)
            for h in range(Z // LANE):
                r, c = at(t, h)
                for v in range(5):
                    total = base[0, v, y, r, c] + div[v][h]
                    if first:
                        total = src[0, v, y, r, c] - (0.5 * segment_step) * total
                    base[0, v, y, r, c] = total
        return carry

    if first:
        spread(src, split)
    lax.fori_loop(0, Y, row, 0)


def spread(src, split):
    _, V, Y, X, _ = src.shape
    groups = split.shape[0]
    xl = X // groups
    per = max(1, SUB // xl)

    def rows(i, carry):
        for v in range(V):
            for g in range(groups):
                parts = [src[0, v, i * per + j, pl.ds(g * xl, xl), :] for j in range(per)]
                split[g, 0, v, pl.ds(pl.multiple_of(i * per * xl, SUB), per * xl), :] = jnp.concatenate(parts, axis=0)
        return carry

    lax.fori_loop(0, Y // per, rows, 0)


def y_kernel(first, *refs):
    prim, low, high, base, out = refs
    _, _, Y, X, Z = prim.shape

    for t, h in tiles(X, Z):
        r, c = at(t, h)

        def load(j):
            if j < 0:
                w = [low[0, v, 2 + j, r, c] for v in range(5)]
            elif j >= Y:
                w = [high[0, v, j - Y, r, c] for v in range(5)]
            else:
                return [prim[0, v, j, r, c] for v in range(5)]
            return primitive(w) if first else w

        here, ahead = load(-2), load(-1)
        d = [0.5 * (a - w) for a, w in zip(ahead, here)]
        left = before = None
        for j in range(-1, Y + 1):
            here, ahead = ahead, load(j + 1)
            back, d = d, [0.5 * (a - w) for a, w in zip(ahead, here)]
            s = [minmod(x, y) for x, y in zip(back, d)]
            if j >= 0:
                right = physical([w - x for w, x in zip(here, s)], 1)
                flux = face(left, right)
                if j >= 1:
                    total = [b - a for a, b in zip(before, flux)]
                    if first:
                        q = [base[0, v, j - 1, r, c] - (0.5 * segment_step) * total[v] for v in range(5)]
                        w = primitive(q)
                        for v in range(5):
                            out[0, v, j - 1, r, c] = w[v]
                    else:
                        groups = out.shape[0]
                        xl = X // groups
                        for v in range(5):
                            val = 0.5 * (base[0, v, j - 1, r, c] + total[v])
                            for part in range(SUB // xl):
                                g = t * (SUB // xl) + part
                                out[g, 0, v, pl.ds((j - 1) * xl, xl), c] = val[part * xl:(part + 1) * xl]
                before = flux
            if j < Y:
                left = physical([w + x for w, x in zip(here, s)], 1)


def combine(terms):
    total = None
    for coef, val in terms:
        if abs(coef) < 1e-9:
            continue
        neg = coef < 0
        term = val if abs(abs(coef) - 1.0) < 1e-9 else val * abs(coef)
        if total is None:
            total = -term if neg else term
        else:
            total = total - term if neg else total + term
    return total


def forward_sums(x):
    N = len(x)
    M, Q = N // 2, N // 4
    even = [None] + [x[n] + x[N - n] for n in range(1, M)]
    odd = [None] + [x[n] - x[N - n] for n in range(1, M)]
    ends = (x[0] + x[M], x[0] - x[M])
    es = [None] + [even[n] + even[M - n] for n in range(1, Q)]
    ed = [None] + [even[n] - even[M - n] for n in range(1, Q)]
    os = [None] + [odd[n] + odd[M - n] for n in range(1, Q)]
    od = [None] + [odd[n] - odd[M - n] for n in range(1, Q)]
    cosine, sine = [], [None]
    for h in range(M + 1):
        src = ed if h % 2 else es
        terms = [(1.0, ends[h % 2])] + [(math.cos(2 * math.pi * h * n / N), src[n]) for n in range(1, Q)]
        if h % 2 == 0:
            terms.append((math.cos(math.pi * h / 2), even[Q]))
        cosine.append(combine(terms))
    for h in range(1, M):
        src = os if h % 2 else od
        terms = [(math.sin(2 * math.pi * h * n / N), src[n]) for n in range(1, Q)]
        if h % 2:
            terms.append((math.sin(math.pi * h / 2), odd[Q]))
        sine.append(combine(terms))
    return cosine, sine


def inverse_sums(a, b):
    M = len(a)
    N, Q = 2 * M, M // 2
    x = [None] * N
    for n in range(Q + 1):
        c = lambda k: math.cos(2 * math.pi * k * n / N)
        s = lambda k: math.sin(2 * math.pi * k * n / N)
        ce = combine([(1.0, a[0]), (1.0 if n % 2 == 0 else -1.0, b[0])] + [(c(k), a[k]) for k in range(2, M, 2)])
        co = combine([(c(k), a[k]) for k in range(1, M, 2)])
        se = combine([(s(k), b[k]) for k in range(2, M, 2)])
        so = combine([(s(k), b[k]) for k in range(1, M, 2)])
        add = lambda p, q: p if q is None else (q if p is None else p + q)
        sub = lambda p, q: p if q is None else (-q if p is None else p - q)
        cp, cm = add(ce, co), sub(ce, co)
        sp, sm = add(so, se), sub(so, se)
        x[n] = add(cp, sp)
        if n > 0:
            x[N - n] = sub(cp, sp)
        if n != M - n:
            x[M - n] = add(cm, sm)
            if M - n < M:
                x[M + n] = sub(cm, sm)
    return x


def rhs_kernel(rates, res, st, out, low, high):
    N, _, rows, Z = res.shape
    K, _, Y, _, _ = out.shape
    xl = rows // Y
    halo = low.shape[2]
    per = max(1, SUB // xl)
    height = per * xl

    def put(k, y, half, val, c):
        place = pl.ds(half * xl, xl)
        out[k, 0, y, place, c] = val
        if y < halo:
            low[k, 0, y, place, c] = val
        if y >= Y - halo:
            high[k, 0, y - (Y - halo), place, c] = val

    for tile in range(rows // height):
        for h in range(Z // LANE):
            c = pl.ds(h * LANE, LANE)
            r = pl.ds(tile * height, height)
            rc, rs = forward_sums([res[n, 0, r, c] for n in range(N)])
            sc, ss = forward_sums([st[n, 0, r, c] for n in range(N)])
            for k in range(K):
                w = rates[k]
                if k == 0:
                    ra, rb, sa, sb, scale = rc[0], rc[K], sc[0], sc[K], -1.0 / N
                else:
                    ra, rb, sa, sb, scale = rc[k], rs[k], sc[k], ss[k], -2.0 / N
                a = scale * (ra + w * sb)
                b = scale * (rb - w * sa)
                for i in range(per):
                    y = tile * per + i
                    put(k, y, 0, a[i * xl:(i + 1) * xl], c)
                    put(k, y, 1, b[i * xl:(i + 1) * xl], c)


def smooth_kernel(rates, core, low, high, out, corr):
    K, _, Y, two, Z = core.shape
    xl = two // 2
    N = 2 * K
    halo = low.shape[2]
    nh = Z // LANE
    lane = lax.broadcasted_iota(jnp.int32, (two, LANE), 1)
    head, tail = lane == 0, lane == LANE - 1
    half = lax.broadcasted_iota(jnp.int32, (two, LANE), 0) < xl
    zero = jnp.zeros((two, LANE), jnp.float32)

    def pair(k, carry):
        w = rates[k]
        det = jnp.full((two, LANE), diagonal_weight * diagonal_weight, jnp.float32) + w * w
        inv = 1.0 / det
        straight = diagonal_weight * inv
        cross = jnp.where(half, -w, w) * inv

        def solve(v):
            other = jnp.concatenate([v[xl:], v[:xl]], axis=0)
            return straight * v + cross * other

        def load(y, h):
            c = pl.ds(h * LANE, LANE)
            if y < 0:
                return low[k, 0, halo + y, :, c]
            if y >= Y:
                return high[k, 0, y - Y, :, c]
            return core[k, 0, y, :, c]

        first = {y: [solve(load(y, h)) for h in range(nh)] for y in range(-halo, Y + halo)}
        cur = first
        for it in range(1, sweeps + 1):
            nxt = {}
            for y in range(-halo + it, Y + halo - it):
                mid = cur[y]
                right = [pltpu.roll(m, LANE - 1, 1) for m in mid]
                left = [pltpu.roll(m, 1, 1) for m in mid]
                row = []
                for h in range(nh):
                    fwd = jnp.where(tail, right[h + 1] if h + 1 < nh else zero, right[h])
                    bwd = jnp.where(head, left[h - 1] if h > 0 else zero, left[h])
                    nb = (cur[y - 1][h] + cur[y + 1][h]) + (fwd + bwd)
                    row.append(first[y][h] + solve(smooth_weight * nb))
                nxt[y] = row
            cur = nxt
        for y in range(Y):
            for h in range(nh):
                corr[k, h, pl.ds(y * two, two), :] = cur[y][h]
        return carry

    lax.fori_loop(0, K, pair, 0)
    for x in range(xl):
        for h in range(nh):
            c = pl.ds(h * LANE, LANE)
            a = [corr[k, h, pl.ds(x, Y, stride=two), :] for k in range(K)]
            b = [corr[k, h, pl.ds(xl + x, Y, stride=two), :] for k in range(K)]
            vals = inverse_sums(a, b)
            for n in range(N):
                out[n, 0, x, :, c] = vals[n]


def struct(*shape):
    return jax.ShapeDtypeStruct(shape, jnp.float32)


def params():
    return pltpu.CompilerParams(dimension_semantics=("arbitrary",))


def by_instance(*shape):
    return pl.BlockSpec((1,) + shape, lambda n: (n,) + (0,) * len(shape))


def second(*shape):
    return pl.BlockSpec((shape[0], 1) + shape[1:], lambda n: (0, n) + (0,) * (len(shape) - 1))


def cost(points, flops, arrays):
    return pl.CostEstimate(flops=points * flops, bytes_accessed=points * 4 * arrays, transcendentals=0)


def xz_call(src, first, groups):
    n, V, Y, X, Z = src.shape
    xl = X // groups
    field = by_instance(V, Y, X, Z)
    outs, specs = [src.shape], [field]
    if first:
        outs = [src.shape, src.shape, (groups, n, V, Y * xl, Z)]
        specs = [field, field, second(groups, V, Y * xl, Z)]
    return pl.pallas_call(
        partial(xz_kernel, first),
        grid=(n,),
        in_specs=[field],
        out_specs=specs,
        out_shape=[struct(*s) for s in outs],
        compiler_params=params(),
        cost_estimate=cost(n * Y * X * Z, 400, 4 * V),
        name="sweep_xz_first" if first else "sweep_xz_second",
    )(src)


def y_call(prim, low, high, base, first, groups):
    n, V, Y, X, Z = prim.shape
    xl = X // groups
    field = by_instance(V, Y, X, Z)
    edge = by_instance(V, 2, X, Z)
    return pl.pallas_call(
        partial(y_kernel, first),
        grid=(n,),
        in_specs=[field, edge, edge, field],
        out_specs=field if first else second(groups, V, Y * xl, Z),
        out_shape=struct(*prim.shape) if first else struct(groups, n, V, Y * xl, Z),
        compiler_params=params(),
        cost_estimate=cost(n * Y * X * Z, 200, 3 * V),
        name="sweep_y_first" if first else "sweep_y_second",
    )(prim, low, high, base)


def rhs_call(rates, res, st, Y):
    N, V, rows, Z = res.shape
    K, xl = N // 2, rows // Y
    field = second(N, rows, Z)
    smem = pl.BlockSpec(memory_space=pltpu.SMEM)
    return pl.pallas_call(
        rhs_kernel,
        grid=(V,),
        in_specs=[smem, field, field],
        out_specs=[second(K, Y, 2 * xl, Z), second(K, sweeps, 2 * xl, Z), second(K, sweeps, 2 * xl, Z)],
        out_shape=[struct(K, V, Y, 2 * xl, Z), struct(K, V, sweeps, 2 * xl, Z), struct(K, V, sweeps, 2 * xl, Z)],
        compiler_params=params(),
        cost_estimate=cost(N * V * rows * Z, 20, 3),
        name="right_hand",
    )(rates, res, st)


def smooth_call(rates, core, low, high):
    K, V, Y, two, Z = core.shape
    xl = two // 2
    smem = pl.BlockSpec(memory_space=pltpu.SMEM)
    edge = second(K, sweeps, two, Z)
    return pl.pallas_call(
        smooth_kernel,
        grid=(V,),
        in_specs=[smem, second(K, Y, two, Z), edge, edge],
        out_specs=second(2 * K, xl, Y, Z),
        out_shape=struct(2 * K, V, xl, Y, Z),
        scratch_shapes=[pltpu.VMEM((K, Z // LANE, Y * two, LANE), jnp.float32)],
        compiler_params=params(),
        cost_estimate=cost(2 * K * V * xl * Y * Z, 60, 3),
        name="smooth",
    )(rates, core, low, high)


def halos(head, tail):
    count = lax.axis_size("blk")
    low = lax.ppermute(tail, "blk", [(i, (i + 1) % count) for i in range(count)])
    high = lax.ppermute(head, "blk", [((i + 1) % count, i) for i in range(count)])
    return low, high


def exchange(x):
    return lax.all_to_all(x, "inst", split_axis=0, concat_axis=0, tiled=True)


def body(state, multiples):
    groups = lax.axis_size("inst")
    n, V, X, Y, Z = state.shape
    N, xl = n * groups, X // groups
    rates = jnp.concatenate([jnp.zeros((1,), jnp.float32), base_rate * multiples.astype(jnp.float32)])

    turn = lambda a: jnp.transpose(a, (0, 1, 3, 2, 4))
    own, head, tail = lax.optimization_barrier((state, turn(state[:, :, :, :2]), turn(state[:, :, :, Y - 2:])))
    low, high = halos(head, tail)
    prim, base, split = xz_call(turn(own), True, groups)
    prim2 = y_call(prim, low, high, base, True, groups)

    low, high = halos(prim2[:, :, :2], prim2[:, :, Y - 2:])
    st = exchange(split).reshape(N, V, Y * xl, Z)
    (base2,) = xz_call(prim2, False, groups)
    second_sweep = y_call(prim2, low, high, base2, False, groups)
    res = exchange(second_sweep).reshape(N, V, Y * xl, Z)

    core, head, tail = rhs_call(rates, res, st, Y)
    low, high = halos(head, tail)
    change = smooth_call(rates, core, low, high)
    back = exchange(change.reshape(groups, n, V, xl, Y, Z))
    return jnp.transpose(back, (1, 2, 0, 3, 4, 5)).reshape(state.shape)


def solution(mesh):
    return jax.shard_map(
        body,
        mesh=mesh,
        in_specs=(P("inst", None, None, "blk", None), P()),
        out_specs=P("inst", None, None, "blk", None),
        check_vma=False,
    )
```

time: 400 us -> 247 us (0.62); the launches traced: 394 us -> 246 us
  other arithmetic: 104 us -> 0.59 us
  local copies, waits for them, and re-layouts: 113 us -> 13.7 us
  Pallas kernels: 0 us -> 60 us
  matrix products: 11.2 us -> 0 us
  waiting for transfers between devices: 104 us -> 113 us
    pallas_call x0 -> x6, Pallas kernels: none -> 60 us  [the longest x2 26.8 us: xz_call(): pl.pallas_call(partial(xz_kernel, first), grid=(n,), in_specs=[field], ou...]
    sub x49 -> x0, other arithmetic: 54.6 us -> none  [the longest x20 44 us: divergence(): 0.5 * (left_flux[member] + right_flux[member])]
    slice x69 -> x2, local copies, waits for them, and re-layouts: 50.1 us -> 5.71 us  [the longest x1 3.2 us: body(): state[:, :, :, Y - 2:]]
    reshape x43 -> x0, local copies, waits for them, and re-layouts: 24.9 us -> none  [the longest x20 17.8 us: residual(): jnp.pad(component, ((0, 0), (0, 0), (0, 0), (2, 2)), mode='edge')]
    unnamed x212 -> x14, local copies, waits for them, and re-layouts: 26.6 us -> 2.45 us
    add x34 -> x0, other arithmetic: 18.1 us -> none  [the longest x30 13.4 us: limited(): jnp.maximum(0.0, jnp.minimum(lower, upper))]
    concatenate x23 -> x1, other arithmetic: 18.4 us -> 0.59 us  [body(): jnp.concatenate([jnp.zeros((1,), jnp.float32), base_rate * multiples.asty...]
    all_to_all x2, waiting for transfers between devices: 16.2 us -> 30.7 us  [exchange(): return lax.all_to_all(x, 'inst', split_axis=0, concat_axis=0, tiled=True)]
  transfers between devices with their start and end apart: 8 -> 8, of which waited for: 7 -> 7; matrix products, arithmetic and copies ran while one was open for 25% -> 1% of each run, Pallas kernels for 0% -> 10%
where the time goes in v1:
time: 247 us; the launch traced here: 246 us
  waiting for transfers between devices  113 us (46%)
  Pallas kernels  60 us (24%)
  blocking collectives  34.9 us (14%)
  starting transfers between devices  23.8 us (10%)
  local copies, waits for them, and re-layouts  13.7 us (6%)
    ppermute x3, waiting for transfers between devices, halos(): lax.ppermute(tail, 'blk', [(i, (i + 1) % count) for i in range(count)])  75.2 us
    all_to_all x1, blocking collectives, exchange(): return lax.all_to_all(x, 'inst', split_axis=0, concat_axis=0, tiled=True)  34.9 us
    all_to_all x2, waiting for transfers between devices, exchange(): return lax.all_to_all(x, 'inst', split_axis=0, concat_axis=0, tiled=True)  30.7 us
    pallas_call x2, Pallas kernels, xz_call(): pl.pallas_call(partial(xz_kernel, first), grid=(n,), in_specs=[field], ou...  26.8 us
    pallas_call x1, Pallas kernels, smooth_call(): pl.pallas_call(smooth_kernel, grid=(V,), in_specs=[smem, second(K, Y, two...  14 us
    pallas_call x2, Pallas kernels, y_call(): pl.pallas_call(partial(y_kernel, first), grid=(n,), in_specs=[field, edge...  12.2 us
    ppermute x3, starting transfers between devices, halos(): lax.ppermute(head, 'blk', [((i + 1) % count, i) for i in range(count)])  10.7 us
    all_to_all x2, starting transfers between devices, exchange(): return lax.all_to_all(x, 'inst', split_axis=0, concat_axis=0, tiled=True)  8.79 us
  transfers between devices with their start and end apart: 8, of which 7 were waited for; matrix products, arithmetic and copies ran while one was open for 1% of the time, Pallas kernels for 10%

profile of v1, /device:TPU:0, one launch (start us, length us, event | category | flops | bytes accessed | tf_op | source)
XLA Modules:
  0.0 246.3 jit_solution(12417531871848101414)
XLA Ops:
  0.0 3.2 %fusion.1 = (f32[4,5,16,2,256]{4,3,2,1,0:T(2,128)S(1)}, f32[4,5,16,2,256]{4,3,2,1,0:T(2,128)S(1)}) fusion(f32[4,5,16,8,256]{4,3,2,1,0:T(8,128)} %param.2), kind=kLoop, calls=%fused_computation.6 | loop fusion | bytes 2621440 | tf_op jit(solution)/shard_map/slice | solution.py:484
  3.2 1.3 copy_bitcast_fusion.1
  4.5 2.4 copy.12
  6.9 13.7 %sweep_xz_first.1 = (f32[4,5,8,16,256]{4,3,2,1,0:T(8,128)}, f32[4,5,8,16,256]{4,3,2,1,0:T(8,128)}, f32[4,4,5,32,256]{4,3,2,1,0:T(8,128)}) custom-call(f32[4,5,8,16,256]{4,3,2,1,0:T(8,128)} %bitcast.14), custom_call_target="tpu_custom_call" | custom-call | flops 52428800 | bytes 10485760 | tf_op jit(solution)/shard_map/sweep_xz_first/pallas_call | solution.py:402
  20.6 4.2 %all-to-all-start.1 = ((f32[4,4,5,32,256]{4,3,2,1,0:T(8,128)}), f32[4,4,5,32,256]{4,3,2,1,0:T(8,128)S(1)}, u32[]{:S(2)}, u32[]{:S(2)}) async-start(f32[4,4,5,32,256]{4,3,2,1,0:T(8,128)} %get-tuple-element.19), calls=%async_computation.1 | async-start | bytes 5242880 | tf_op jit(solution)/shard_map/all_to_all | solution.py:474
  24.8 2.5 %collective-permute-start = (f32[4,5,2,16,256]{4,3,2,1,0:T(8,128)}, f32[4,5,2,16,256]{4,3,2,1,0:T(8,128)S(1)}, u32[]{:S(2)}, u32[]{:S(2)}) collective-permute-start(f32[4,5,2,16,256]{4,3,2,1,0:T(8,128)} %get-tuple-element.16), channel_id=1, source_target_pairs={{0,1},{1,2},{2,3},{3,4},{4,5},{5,6},{6,7},{7,0},{8,9},{9,10},{10,1... | collective-permute-start | bytes 1966088 | tf_op jit(solution)/shard_map/ppermute | solution.py:468
  27.3 3.1 %collective-permute-start.1 = (f32[4,5,2,16,256]{4,3,2,1,0:T(8,128)}, f32[4,5,2,16,256]{4,3,2,1,0:T(8,128)}, u32[]{:S(2)}, u32[]{:S(2)}) collective-permute-start(f32[4,5,2,16,256]{4,3,2,1,0:T(8,128)} %get-tuple-element.17), channel_id=1, source_target_pairs={{1,0},{2,1},{3,2},{4,3},{5,4},{6,5},{7,6},{0,7},{9,8},{10,9},{11,1... | collective-permute-start | bytes 1966088 | tf_op jit(solution)/shard_map/ppermute | solution.py:469
  30.4 25.8 %collective-permute-done.refs_1_ = f32[4,5,2,16,256]{4,3,2,1,0:T(8,128)S(1)} collective-permute-done((f32[4,5,2,16,256]{4,3,2,1,0:T(8,128)}, f32[4,5,2,16,256]{4,3,2,1,0:T(8,128)S(1)}, u32[]{:S(2)}, u32[]{:S(2)}) %collective-permute-start) | collective-permute-done | bytes 655392 | tf_op jit(solution)/shard_map/ppermute | solution.py:468
  56.3 2.2 collective-permute-done.1.refs_2_
  58.5 6.2 %sweep_y_first.1.refs_0_ = f32[4,5,8,16,256]{4,3,2,1,0:T(8,128)} custom-call(f32[4,5,8,16,256]{4,3,2,1,0:T(8,128)} %get-tuple-element.15.refs_0_, f32[4,5,2,16,256]{4,3,2,1,0:T(8,128)} %copy-done.4, f32[4,5,2,16,256]{4,3,2,1,0:T(8,128)} %collective-permute-done.1.refs_2_, f32[4,5,8,16,256]{4,3,2,1,0:T(8,128)} %get-tuple-element.18.refs_3_), custom_call_target="tpu_custom_call" | custom-call | flops 26214400 | bytes 7864320 | tf_op jit(solution)/shard_map/sweep_y_first/pallas_call | solution.py:419
  64.6 2.5 %fusion = (f32[4,5,2,16,256]{4,3,2,1,0:T(8,128)}, f32[4,5,2,16,256]{4,3,2,1,0:T(8,128)}) fusion(f32[4,5,8,16,256]{4,3,2,1,0:T(8,128)} %sweep_y_first.1.refs_0_), kind=kLoop, calls=%fused_computation.5 | loop fusion | bytes 2621440 | tf_op jit(solution)/shard_map/slice | solution.py:489
  67.1 1.1 collective-permute-start.2
  68.2 3.6 %collective-permute-start.3 = (f32[4,5,2,16,256]{4,3,2,1,0:T(8,128)}, f32[4,5,2,16,256]{4,3,2,1,0:T(8,128)}, u32[]{:S(2)}, u32[]{:S(2)}) collective-permute-start(f32[4,5,2,16,256]{4,3,2,1,0:T(8,128)} %get-tuple-element.23), channel_id=1, source_target_pairs={{1,0},{2,1},{3,2},{4,3},{5,4},{6,5},{7,6},{0,7},{9,8},{10,9},{11,1... | collective-permute-start | bytes 1966088 | tf_op jit(solution)/shard_map/ppermute | solution.py:469
  71.9 13.1 %sweep_xz_second.1.refs_3_ = f32[4,5,8,16,256]{4,3,2,1,0:T(8,128)} custom-call(f32[4,5,8,16,256]{4,3,2,1,0:T(8,128)} %sweep_y_first.1.refs_0_), custom_call_target="tpu_custom_call" | custom-call | flops 52428800 | bytes 10485760 | tf_op jit(solution)/shard_map/sweep_xz_second/pallas_call | solution.py:402
  85.0 11.3 %collective-permute-done.2.refs_1_ = f32[4,5,2,16,256]{4,3,2,1,0:T(8,128)S(1)} collective-permute-done((f32[4,5,2,16,256]{4,3,2,1,0:T(8,128)}, f32[4,5,2,16,256]{4,3,2,1,0:T(8,128)S(1)}, u32[]{:S(2)}, u32[]{:S(2)}) %collective-permute-start.2) | collective-permute-done | bytes 655392 | tf_op jit(solution)/shard_map/ppermute | solution.py:468
  96.3 2.6 %collective-permute-done.3.refs_2_ = f32[4,5,2,16,256]{4,3,2,1,0:T(8,128)} collective-permute-done((f32[4,5,2,16,256]{4,3,2,1,0:T(8,128)}, f32[4,5,2,16,256]{4,3,2,1,0:T(8,128)}, u32[]{:S(2)}, u32[]{:S(2)}) %collective-permute-start.3) | collective-permute-done | bytes 655392 | tf_op jit(solution)/shard_map/ppermute | solution.py:469
  98.8 6.1 %sweep_y_second.1 = f32[4,4,5,32,256]{4,3,2,1,0:T(8,128)} custom-call(f32[4,5,8,16,256]{4,3,2,1,0:T(8,128)} %sweep_y_first.1.refs_0_, f32[4,5,2,16,256]{4,3,2,1,0:T(8,128)} %copy-done.5, f32[4,5,2,16,256]{4,3,2,1,0:T(8,128)} %collective-permute-done.3.refs_2_, f32[4,5,8,16,256]{4,3,2,1,0:T(8,128)} %sweep_xz_second.1.refs_3_), custom_call_target="tpu_custom_call" | custom-call | flops 26214400 | bytes 7864320 | tf_op jit(solution)/shard_map/sweep_y_second/pallas_call | solution.py:419
  104.9 0.0 all-to-all-done.1
  104.9 0.0 copy-start
  104.9 1.5 copy-done
  106.4 4.6 %all-to-all-start = ((f32[4,4,5,32,256]{4,3,2,1,0:T(8,128)}), f32[4,4,5,32,256]{4,3,2,1,0:T(8,128)}, u32[]{:S(2)}, u32[]{:S(2)}) async-start(f32[4,4,5,32,256]{4,3,2,1,0:T(8,128)} %sweep_y_second.1), calls=%async_computation | async-start | bytes 5242880 | tf_op jit(solution)/shard_map/all_to_all | solution.py:474
  111.0 0.6 pad_maximum_fusion.rates
  111.6 30.7 %all-to-all-done = f32[4,4,5,32,256]{4,3,2,1,0:T(8,128)} async-done(((f32[4,4,5,32,256]{4,3,2,1,0:T(8,128)}), f32[4,4,5,32,256]{4,3,2,1,0:T(8,128)}, u32[]{:S(2)}, u32[]{:S(2)}) %all-to-all-start) | async-done | bytes 2621472 | tf_op jit(solution)/shard_map/all_to_all | solution.py:474
  142.3 7.0 %right_hand.1 = (f32[8,5,8,8,256]{4,3,2,1,0:T(8,128)}, f32[8,5,3,8,256]{4,3,2,1,0:T(8,128)}, f32[8,5,3,8,256]{4,3,2,1,0:T(8,128)}) custom-call(f32[8]{0:T(128)} %pad_maximum_fusion.rates, f32[16,5,32,256]{3,2,1,0:T(8,128)} %bitcast.3.res, f32[16,5,32,256]{3,2,1,0:T(8,128)} %bitcast.13), custom_call_target="tpu_custom_call" | custom-call | flops 13107200 | bytes 7864320 | tf_op jit(solution)/shard_map/right_hand/pallas_call | solution.py:436
  149.3 0.7 collective-permute-start.4
  150.0 4.0 %collective-permute-start.5 = (f32[8,5,3,8,256]{4,3,2,1,0:T(8,128)}, f32[8,5,3,8,256]{4,3,2,1,0:T(8,128)S(1)}, u32[]{:S(2)}, u32[]{:S(2)}) collective-permute-start(f32[8,5,3,8,256]{4,3,2,1,0:T(8,128)} %get-tuple-element.22), channel_id=1, source_target_pairs={{1,0},{2,1},{3,2},{4,3},{5,4},{6,5},{7,6},{0,7},{9,8},{10,9},{11,1... | collective-permute-start | bytes 2949128 | tf_op jit(solution)/shard_map/ppermute | solution.py:469
  154.0 38.1 %collective-permute-done.4.low = f32[8,5,3,8,256]{4,3,2,1,0:T(8,128)S(1)} collective-permute-done((f32[8,5,3,8,256]{4,3,2,1,0:T(8,128)}, f32[8,5,3,8,256]{4,3,2,1,0:T(8,128)S(1)}, u32[]{:S(2)}, u32[]{:S(2)}) %collective-permute-start.4) | collective-permute-done | bytes 983072 | tf_op jit(solution)/shard_map/ppermute | solution.py:468
  192.1 2.5 %collective-permute-done.5.high = f32[8,5,3,8,256]{4,3,2,1,0:T(8,128)S(1)} collective-permute-done((f32[8,5,3,8,256]{4,3,2,1,0:T(8,128)}, f32[8,5,3,8,256]{4,3,2,1,0:T(8,128)S(1)}, u32[]{:S(2)}, u32[]{:S(2)}) %collective-permute-start.5) | collective-permute-done | bytes 983072 | tf_op jit(solution)/shard_map/ppermute | solution.py:469
  194.7 0.9 copy-done.3
  195.6 14.0 %smooth.1 = f32[16,5,4,8,256]{4,3,2,1,0:T(8,128)} custom-call(f32[8]{0:T(128)} %pad_maximum_fusion.rates, f32[8,5,8,8,256]{4,3,2,1,0:T(8,128)} %get-tuple-element.20.core, f32[8,5,3,8,256]{4,3,2,1,0:T(8,128)} %copy-done.2, f32[8,5,3,8,256]{4,3,2,1,0:T(8,128)} %copy-done.3), custom_call_target="tpu_custom_call" | custom-call | flops 39321600 | bytes 7864320 | tf_op jit(solution)/shard_map/smooth/pallas_call | solution.py:453
  209.6 34.9 %all_to_all.15 = f32[4,4,5,4,8,256]{5,4,3,2,1,0:T(8,128)S(1)} all-to-all(f32[4,4,5,4,8,256]{5,4,3,2,1,0:T(8,128)} %bitcast.12), channel_id=1, replica_groups=mesh['inst'=4,'blk'=8] {'inst'}, dimensions={0} | all-to-all | bytes 5242880 | tf_op jit(solution)/shard_map/all_to_all | solution.py:474
  244.5 1.8 copy.6
  (12 shorter events, 0.0 us)
Async XLA Ops:
  0.0 4.5 %copy-start.1 = (f32[4,5,16,8,256]{4,3,2,1,0:T(8,128)S(1)}, f32[4,5,16,8,256]{4,3,2,1,0:T(8,128)}, u32[]{:S(2)}) copy-start(f32[4,5,16,8,256]{4,3,2,1,0:T(8,128)} %param.2) | copy-start | bytes 7864324
  20.6 84.3 %all-to-all-start.1 = ((f32[4,4,5,32,256]{4,3,2,1,0:T(8,128)}), f32[4,4,5,32,256]{4,3,2,1,0:T(8,128)S(1)}, u32[]{:S(2)}, u32[]{:S(2)}) async-start(f32[4,4,5,32,256]{4,3,2,1,0:T(8,128)} %get-tuple-element.19), calls=%async_computation.1 | async-start | bytes 5242880 | tf_op jit(solution)/shard_map/all_to_all | solution.py:474
  24.8 31.4 %collective-permute-start = (f32[4,5,2,16,256]{4,3,2,1,0:T(8,128)}, f32[4,5,2,16,256]{4,3,2,1,0:T(8,128)S(1)}, u32[]{:S(2)}, u32[]{:S(2)}) collective-permute-start(f32[4,5,2,16,256]{4,3,2,1,0:T(8,128)} %get-tuple-element.16), channel_id=1, source_target_pairs={{0,1},{1,2},{2,3},{3,4},{4,5},{5,6},{6,7},{7,0},{8,9},{9,10},{10,1... | collective-permute-start | bytes 1966088 | tf_op jit(solution)/shard_map/ppermute | solution.py:468
  27.3 31.1 %collective-permute-start.1 = (f32[4,5,2,16,256]{4,3,2,1,0:T(8,128)}, f32[4,5,2,16,256]{4,3,2,1,0:T(8,128)}, u32[]{:S(2)}, u32[]{:S(2)}) collective-permute-start(f32[4,5,2,16,256]{4,3,2,1,0:T(8,128)} %get-tuple-element.17), channel_id=1, source_target_pairs={{1,0},{2,1},{3,2},{4,3},{5,4},{6,5},{7,6},{0,7},{9,8},{10,9},{11,1... | collective-permute-start | bytes 1966088 | tf_op jit(solution)/shard_map/ppermute | solution.py:469
  56.2 2.2 copy-start.4
  67.1 29.2 %collective-permute-start.2 = (f32[4,5,2,16,256]{4,3,2,1,0:T(8,128)}, f32[4,5,2,16,256]{4,3,2,1,0:T(8,128)S(1)}, u32[]{:S(2)}, u32[]{:S(2)}) collective-permute-start(f32[4,5,2,16,256]{4,3,2,1,0:T(8,128)} %get-tuple-element.24), channel_id=1, source_target_pairs={{0,1},{1,2},{2,3},{3,4},{4,5},{5,6},{6,7},{7,0},{8,9},{9,10},{10,1... | collective-permute-start | bytes 1966088 | tf_op jit(solution)/shard_map/ppermute | solution.py:468
  68.2 30.6 %collective-permute-start.3 = (f32[4,5,2,16,256]{4,3,2,1,0:T(8,128)}, f32[4,5,2,16,256]{4,3,2,1,0:T(8,128)}, u32[]{:S(2)}, u32[]{:S(2)}) collective-permute-start(f32[4,5,2,16,256]{4,3,2,1,0:T(8,128)} %get-tuple-element.23), channel_id=1, source_target_pairs={{1,0},{2,1},{3,2},{4,3},{5,4},{6,5},{7,6},{0,7},{9,8},{10,9},{11,1... | collective-permute-start | bytes 1966088 | tf_op jit(solution)/shard_map/ppermute | solution.py:469
  96.3 2.6 %copy-start.5 = (f32[4,5,2,16,256]{4,3,2,1,0:T(8,128)}, f32[4,5,2,16,256]{4,3,2,1,0:T(8,128)S(1)}, u32[]{:S(2)}) copy-start(f32[4,5,2,16,256]{4,3,2,1,0:T(8,128)S(1)} %collective-permute-done.2.refs_1_) | copy-start | bytes 1966084
  104.9 6.1 %copy-start.6 = (s32[7]{0:T(128)S(1)}, s32[7]{0:T(128)}, u32[]{:S(2)}) copy-start(s32[7]{0:T(128)} %param.3) | copy-start | bytes 88
  104.9 1.5 copy-start
  106.4 35.9 %all-to-all-start = ((f32[4,4,5,32,256]{4,3,2,1,0:T(8,128)}), f32[4,4,5,32,256]{4,3,2,1,0:T(8,128)}, u32[]{:S(2)}, u32[]{:S(2)}) async-start(f32[4,4,5,32,256]{4,3,2,1,0:T(8,128)} %sweep_y_second.1), calls=%async_computation | async-start | bytes 5242880 | tf_op jit(solution)/shard_map/all_to_all | solution.py:474
  149.3 42.8 %collective-permute-start.4 = (f32[8,5,3,8,256]{4,3,2,1,0:T(8,128)}, f32[8,5,3,8,256]{4,3,2,1,0:T(8,128)S(1)}, u32[]{:S(2)}, u32[]{:S(2)}) collective-permute-start(f32[8,5,3,8,256]{4,3,2,1,0:T(8,128)} %get-tuple-element.21), channel_id=1, source_target_pairs={{0,1},{1,2},{2,3},{3,4},{4,5},{5,6},{6,7},{7,0},{8,9},{9,10},{10,1... | collective-permute-start | bytes 2949128 | tf_op jit(solution)/shard_map/ppermute | solution.py:468
  150.0 44.7 %collective-permute-start.5 = (f32[8,5,3,8,256]{4,3,2,1,0:T(8,128)}, f32[8,5,3,8,256]{4,3,2,1,0:T(8,128)S(1)}, u32[]{:S(2)}, u32[]{:S(2)}) collective-permute-start(f32[8,5,3,8,256]{4,3,2,1,0:T(8,128)} %get-tuple-element.22), channel_id=1, source_target_pairs={{1,0},{2,1},{3,2},{4,3},{5,4},{6,5},{7,6},{0,7},{9,8},{10,9},{11,1... | collective-permute-start | bytes 2949128 | tf_op jit(solution)/shard_map/ppermute | solution.py:469
  192.1 2.6 %copy-start.2 = (f32[8,5,3,8,256]{4,3,2,1,0:T(8,128)}, f32[8,5,3,8,256]{4,3,2,1,0:T(8,128)S(1)}, u32[]{:S(2)}) copy-start(f32[8,5,3,8,256]{4,3,2,1,0:T(8,128)S(1)} %collective-permute-done.4.low) | copy-start | bytes 2949124
  194.7 0.9 copy-start.3
